TPU v7x, 32 devices: a whole 2x2x4 slice. The times are simulated.
32 devices in a mesh: dp: 2 (over x), tp: 4 (over z), cp: 4 (over y, core).
Axes of the slice: x: 2, y: 2, z: 4, core: 2. Of those that a mesh axis runs over, the one named last changes fastest.
Arguments:
- hidden: bfloat16 [2, 4096, 3072], P('dp', 'cp'), parts along dimension 0
- cotangent: bfloat16 [2, 4096, 3072], P('dp', 'cp'), parts along dimension 0
- positions: int32 [8192], P(('dp', 'cp')), parts along dimension 0
- w_q: bfloat16 [3072, 3072], P(None, 'tp')
- w_k: bfloat16 [3072, 1024], P(None, 'tp')
- w_v: bfloat16 [3072, 1024], P(None, 'tp')
- w_o: bfloat16 [3072, 3072], P('tp')
- w_pre: float32 [3072], replicated
- w_post: float32 [3072], replicated
- q_norm: float32 [128], replicated
- k_norm: float32 [128], replicated
Outputs:
- output 1: bfloat16 [2, 4096, 3072], P('dp', 'cp'), parts along dimension 0
- output 2: bfloat16 [2, 4096, 3072], P('dp', 'cp'), parts along dimension 0
- output 3: float32 [6144, 3072], P('dp', 'tp'), parts along dimension 0
- output 4: float32 [6144, 1024], P('dp', 'tp'), parts along dimension 0
- output 5: float32 [6144, 1024], P('dp', 'tp'), parts along dimension 0
- output 6: float32 [6144, 3072], P(('dp', 'tp')), parts along dimension 0
- output 7: float32 [6144], P('dp'), parts along dimension 0
- output 8: float32 [6144], P('dp'), parts along dimension 0
- output 9: float32 [256], P('dp'), parts along dimension 0
- output 10: float32 [256], P('dp'), parts along dimension 0
There are 2 independent parts. A program takes and returns all parts, laid end to end along the dimension named above; an argument that names none is the same for every part.
All inputs are finite; a program needn't handle non-finite values.
Results may differ from a plain program's by a relative error of at most 0.02.
Values are sent between devices in bfloat16 or wider.
A program may use at most 1 GiB of HBM per device.

v0:
```python
import jax
import jax.numpy as jnp
from jax import lax
from jax.sharding import PartitionSpec as P

EPS = 1e-6
ROPE_BASE = 1000000.0
ROPE_SCALE = 8.0
NEG_BIG = -1e30


def rms_unit(values):
    inv_rms = lax.rsqrt(jnp.mean(values * values, axis=-1, keepdims=True) + EPS)
    return values * inv_rms, inv_rms


def rms_unit_back(d_unit, unit_vals, inv_rms):
    return inv_rms * (d_unit - unit_vals * jnp.mean(d_unit * unit_vals, axis=-1, keepdims=True))


def rope_tables(pos_loc, head_dim):
    half_dim = head_dim // 2
    inv_freq = 1.0 / (ROPE_SCALE * ROPE_BASE ** (jnp.arange(half_dim, dtype=jnp.float32) * (2.0 / head_dim)))
    angles = pos_loc.astype(jnp.float32)[:, None] * inv_freq[None, :]
    return jnp.cos(angles)[None, :, None, :], jnp.sin(angles)[None, :, None, :]


def rope_apply(values, cos_t, sin_t):
    half_dim = values.shape[-1] // 2
    lower_half = values[..., :half_dim]
    upper_half = values[..., half_dim:]
    return jnp.concatenate([lower_half * cos_t - upper_half * sin_t, upper_half * cos_t + lower_half * sin_t], axis=-1)


def rope_back(grads_in, cos_t, sin_t):
    half_dim = grads_in.shape[-1] // 2
    lower_half = grads_in[..., :half_dim]
    upper_half = grads_in[..., half_dim:]
    return jnp.concatenate([lower_half * cos_t + upper_half * sin_t, upper_half * cos_t - lower_half * sin_t], axis=-1)


def head_norm(raw_heads, norm_gain, cos_t, sin_t):
    unit_vals, inv_rms = rms_unit(raw_heads.astype(jnp.float32))
    final_heads = rope_apply(unit_vals * (1.0 + norm_gain), cos_t, sin_t).astype(jnp.bfloat16)
    return final_heads, unit_vals, inv_rms


def head_norm_back(d_final, norm_gain, unit_vals, inv_rms, cos_t, sin_t):
    d_scaled = rope_back(d_final, cos_t, sin_t)
    d_gain = jnp.sum(d_scaled * unit_vals, axis=(0, 1, 2))
    return rms_unit_back(d_scaled * (1.0 + norm_gain), unit_vals, inv_rms), d_gain


def attend_block(run_stats, q_fin, k_blk, v_blk, q_pos, k_pos, score_scale):
    run_max, run_sum, run_acc = run_stats
    scores = jnp.einsum('bqkgd,bskd->bkgqs', q_fin, k_blk, preferred_element_type=jnp.float32) * score_scale
    allowed = k_pos[None, :] <= q_pos[:, None]
    new_max = jnp.maximum(run_max, jnp.max(jnp.where(allowed, scores, NEG_BIG), axis=-1))
    attn_prob = jnp.where(allowed, jnp.exp(scores - new_max[..., None]), 0.0)
    factor = jnp.exp(run_max - new_max)
    new_sum = run_sum * factor + jnp.sum(attn_prob, axis=-1)
    new_acc = run_acc * factor[..., None] + jnp.einsum('bkgqs,bskd->bkgqd', attn_prob.astype(jnp.bfloat16), v_blk, preferred_element_type=jnp.float32)
    return new_max, new_sum, new_acc


def grad_block(q_fin, d_out, log_norm, row_delta, q_pos, k_blk, v_blk, k_pos, score_scale):
    scores = jnp.einsum('bqkgd,bskd->bkgqs', q_fin, k_blk, preferred_element_type=jnp.float32) * score_scale
    allowed = k_pos[None, :] <= q_pos[:, None]
    attn_prob = jnp.where(allowed, jnp.exp(scores - log_norm[..., None]), 0.0)
    grad_v = jnp.einsum('bkgqs,bkgqd->bskd', attn_prob.astype(jnp.bfloat16), d_out, preferred_element_type=jnp.float32)
    d_prob = jnp.einsum('bkgqd,bskd->bkgqs', d_out, v_blk, preferred_element_type=jnp.float32)
    d_score = (attn_prob * (d_prob - row_delta[..., None]) * score_scale).astype(jnp.bfloat16)
    grad_q = jnp.einsum('bkgqs,bskd->bqkgd', d_score, k_blk, preferred_element_type=jnp.float32)
    grad_k = jnp.einsum('bkgqs,bqkgd->bskd', d_score, q_fin, preferred_element_type=jnp.float32)
    return grad_q, grad_k, grad_v


def solution(mesh):
    n_cp = mesh.shape['cp']
    next_hop = [(dev_idx, (dev_idx + 1) % n_cp) for dev_idx in range(n_cp)]

    def per_device(hidden, cotangent, pos_loc, w_q, w_k, w_v, w_o, w_pre, w_post, q_norm, k_norm):
        head_dim = q_norm.shape[0]
        n_batch, seq_loc, model_dim = hidden.shape
        q_heads = w_q.shape[1] // head_dim
        kv_heads = w_k.shape[1] // head_dim
        groups = q_heads // kv_heads
        score_scale = head_dim ** -0.5
        cos_t, sin_t = rope_tables(pos_loc, head_dim)

        x_f32 = hidden.astype(jnp.float32)
        x_unit, x_inv = rms_unit(x_f32)
        normed = (x_unit * (1.0 + w_pre)).astype(jnp.bfloat16)
        q_raw = jnp.einsum('bsd,dh->bsh', normed, w_q, preferred_element_type=jnp.float32).astype(jnp.bfloat16).reshape(n_batch, seq_loc, q_heads, head_dim)
        k_raw = jnp.einsum('bsd,dh->bsh', normed, w_k, preferred_element_type=jnp.float32).astype(jnp.bfloat16).reshape(n_batch, seq_loc, kv_heads, head_dim)
        v_loc = jnp.einsum('bsd,dh->bsh', normed, w_v, preferred_element_type=jnp.float32).astype(jnp.bfloat16).reshape(n_batch, seq_loc, kv_heads, head_dim)
        q_fin, q_unit, q_inv = head_norm(q_raw, q_norm, cos_t, sin_t)
        k_fin, k_unit, k_inv = head_norm(k_raw, k_norm, cos_t, sin_t)
        q_fin = q_fin.reshape(n_batch, seq_loc, kv_heads, groups, head_dim)

        stat_shape = (n_batch, kv_heads, groups, seq_loc)
        init_stats = (jnp.full(stat_shape, NEG_BIG, jnp.float32), jnp.zeros(stat_shape, jnp.float32), jnp.zeros(stat_shape + (head_dim,), jnp.float32))
        run_stats = attend_block(init_stats, q_fin, k_fin, v_loc, pos_loc, pos_loc, score_scale)

        def fwd_step(step_idx, loop_state):
            k_blk, v_blk, k_pos, carried = loop_state
            k_blk, v_blk, k_pos = lax.ppermute((k_blk, v_blk, k_pos), 'cp', next_hop)
            return k_blk, v_blk, k_pos, attend_block(carried, q_fin, k_blk, v_blk, pos_loc, k_pos, score_scale)

        final_state = lax.fori_loop(0, n_cp - 1, fwd_step, (k_fin, v_loc, pos_loc, run_stats))
        run_max, run_sum, run_acc = final_state[3]
        out_f32 = run_acc / run_sum[..., None]
        log_norm = run_max + jnp.log(run_sum)
        out_bf = out_f32.astype(jnp.bfloat16)
        wo_split = w_o.reshape(kv_heads, groups, head_dim, model_dim)
        attn = lax.psum(jnp.einsum('bkgqd,kgdm->bqm', out_bf, wo_split, preferred_element_type=jnp.float32), 'tp')
        attn_unit, attn_inv = rms_unit(attn)
        output = (x_f32 + attn_unit * (1.0 + w_post)).astype(jnp.bfloat16)

        grad_y = cotangent.astype(jnp.float32)
        d_post = lax.psum(jnp.sum(grad_y * attn_unit, axis=(0, 1)), 'cp')
        d_attn = rms_unit_back(grad_y * (1.0 + w_post), attn_unit, attn_inv).astype(jnp.bfloat16)
        d_wo = lax.psum(jnp.einsum('bkgqd,bqm->kgdm', out_bf, d_attn, preferred_element_type=jnp.float32), 'cp').reshape(q_heads * head_dim, model_dim)
        d_out = jnp.einsum('bqm,kgdm->bkgqd', d_attn, wo_split, preferred_element_type=jnp.float32)
        row_delta = jnp.sum(d_out * out_f32, axis=-1)
        d_out_bf = d_out.astype(jnp.bfloat16)

        dq_first, dk_first, dv_first = grad_block(q_fin, d_out_bf, log_norm, row_delta, pos_loc, k_fin, v_loc, pos_loc, score_scale)

        def bwd_step(step_idx, loop_state):
            k_blk, v_blk, k_pos, dk_run, dv_run, dq_run = loop_state
            k_blk, v_blk, k_pos, dk_run, dv_run = lax.ppermute((k_blk, v_blk, k_pos, dk_run, dv_run), 'cp', next_hop)
            grad_q, grad_k, grad_v = grad_block(q_fin, d_out_bf, log_norm, row_delta, pos_loc, k_blk, v_blk, k_pos, score_scale)
            return k_blk, v_blk, k_pos, dk_run + grad_k, dv_run + grad_v, dq_run + grad_q

        back_state = lax.fori_loop(0, n_cp - 1, bwd_step, (k_fin, v_loc, pos_loc, dk_first, dv_first, dq_first))
        dk_home, dv_home = lax.ppermute((back_state[3], back_state[4]), 'cp', next_hop)
        dq_all = back_state[5].reshape(n_batch, seq_loc, q_heads, head_dim)

        dq_raw, dq_gain = head_norm_back(dq_all, q_norm, q_unit, q_inv, cos_t, sin_t)
        dk_raw, dk_gain = head_norm_back(dk_home, k_norm, k_unit, k_inv, cos_t, sin_t)
        dq_bf = dq_raw.reshape(n_batch, seq_loc, q_heads * head_dim).astype(jnp.bfloat16)
        dk_bf = dk_raw.reshape(n_batch, seq_loc, kv_heads * head_dim).astype(jnp.bfloat16)
        dv_bf = dv_home.reshape(n_batch, seq_loc, kv_heads * head_dim).astype(jnp.bfloat16)
        d_wq = lax.psum(jnp.einsum('bsd,bsh->dh', normed, dq_bf, preferred_element_type=jnp.float32), 'cp')
        d_wk = lax.psum(jnp.einsum('bsd,bsh->dh', normed, dk_bf, preferred_element_type=jnp.float32), 'cp')
        d_wv = lax.psum(jnp.einsum('bsd,bsh->dh', normed, dv_bf, preferred_element_type=jnp.float32), 'cp')
        d_normed = lax.psum(jnp.einsum('bsh,dh->bsd', dq_bf, w_q, preferred_element_type=jnp.float32) + jnp.einsum('bsh,dh->bsd', dk_bf, w_k, preferred_element_type=jnp.float32) + jnp.einsum('bsh,dh->bsd', dv_bf, w_v, preferred_element_type=jnp.float32), 'tp')
        d_qnorm = lax.psum(dq_gain, ('tp', 'cp'))
        d_knorm = lax.psum(dk_gain, ('tp', 'cp'))
        d_pre = lax.psum(jnp.sum(d_normed * x_unit, axis=(0, 1)), 'cp')
        d_hidden = (grad_y + rms_unit_back(d_normed * (1.0 + w_pre), x_unit, x_inv)).astype(jnp.bfloat16)
        return output, d_hidden, d_wq, d_wk, d_wv, d_wo, d_pre, d_post, d_qnorm, d_knorm

    specs_in = (P('dp', 'cp', None), P('dp', 'cp', None), P(('dp', 'cp')), P(None, 'tp'), P(None, 'tp'), P(None, 'tp'), P('tp', None), P(None), P(None), P(None), P(None))
    specs_out = (P('dp', 'cp', None), P('dp', 'cp', None), P('dp', 'tp'), P('dp', 'tp'), P('dp', 'tp'), P(('dp', 'tp'), None), P('dp'), P('dp'), P('dp'), P('dp'))
    return jax.shard_map(per_device, mesh=mesh, in_specs=specs_in, out_specs=specs_out, check_vma=False)
```

profile of v0, /device:TPU:0, one launch (start us, length us, event | category | flops | bytes accessed | tf_op | source)
XLA Modules:
  0.0 1951.4 jit_solution(15166954128807944678)
XLA Ops:
  37.4 8.6 fusion.101
  53.6 13.0 fusion.57
  66.6 11.5 fusion.64
  78.2 13.6 add_bitcast_fusion.1
  92.7 151.5 %while.40 = (s32[]{:T(128)}, bf16[1,1024,2,128]{3,1,2,0:T(8,128)(2,1)}, bf16[1,1024,2,128]{3,1,2,0:T(8,128)(2,1)}, s32[1024]{0:T(1024)S(1)}, f32[1,2,3,1024]{3,2...) while((s32[]{:T(128)}, ...), condition=%wide.region_8.9_spmd, body=%wide.region_5.8_spmd.sunk | while | flops 3293071360 | bytes 95322328 | solution.py:110
  102.8 11.6 fusion.181
  114.5 11.4 fusion.183
  129.7 14.1 bitcast_add_fusion.8
  153.1 11.6 fusion.181
  164.7 11.4 fusion.183
  179.9 14.1 bitcast_add_fusion.8
  203.3 11.6 fusion.181
  215.0 11.4 fusion.183
  230.2 14.1 bitcast_add_fusion.8
  247.8 10.6 convolution_bitcast_fusion
  260.3 424.6 %all-reduce.7.cloned.1.call-done = f32[1,1024,3072]{2,1,0:T(8,128)} async-done(((f32[1,1024,3072]{2,1,0:T(8,128)}), f32[1,1024,3072]{2,1,0:T(8,128)}) %all-reduce.7.cloned.1.call-update) | async-done | bytes 12582928 | tf_op jit(solution)/shard_map/psum | solution.py:116
  690.5 9.9 fusion.82
  700.5 13.8 fusion.93
  721.7 12.5 fusion.105
  734.2 20.2 %fusion.85 = bf16[2,3,1024,1024]{2,3,1,0:T(8,128)(2,1)} fusion(f32[2,1024,1024,3]{2,1,3,0:T(8,128)} %get-tuple-element.297, f32[2,3,1024]{2,1,0:T(4,128)S(1)} %get-tuple-element.298, f32[2,3,1024]{2,1,0:T(4,128)S(1)} %bitcast.489, pred[1024,1024]{0,1:T(8,128)(4,1)} %broadcast_compare_fusion.2, bf16[1024,2,128,1]{0,2,3,1:T(8,128)(2,1)} %bitcast.486, ...), kind=kOutput, calls=%fused_computation.90 | convolution fusion | flops 1654652928 | bytes 40943616 | tf_op jit(solution)/shard_map/bkgqd,bskd->bkgqs/dot_general | solution.py:71
  754.4 11.4 convolution_bitcast_fusion.2
  765.7 8.2 convolution_bitcast_fusion.1
  785.2 229.8 %while.41 = (s32[]{:T(128)}, bf16[1,1024,2,128]{3,1,2,0:T(8,128)(2,1)}, bf16[1,1024,2,128]{3,1,2,0:T(8,128)(2,1)}, s32[1024]{0:T(1024)S(1)}, f32[1,1024,2,128]{3...) while((s32[]{:T(128)}, ...), condition=%wide.region_14.15_spmd, body=%wide.region_13.14_spmd.sunk | while | flops 8124628992 | bytes 160014736 | solution.py:136
  795.9 12.8 fusion.194
  808.7 16.6 fusion.195
  825.3 11.4 bitcast_add_fusion.9
  840.5 9.4 fusion.196
  849.9 12.1 fusion.197
  872.3 12.8 fusion.194
  885.1 16.6 fusion.195
  901.6 11.4 bitcast_add_fusion.9
  916.8 9.4 fusion.196
  926.2 12.1 fusion.197
  948.7 12.8 fusion.194
  961.5 16.6 fusion.195
  978.0 11.4 bitcast_add_fusion.9
  993.2 9.4 fusion.196
  1002.6 12.1 fusion.197
  1038.3 11.0 fusion.124
  1063.4 14.7 add_bitcast_fusion
  1078.9 10.6 fusion.129
  1089.5 10.3 fusion.126
  1108.3 31.9 %all-reduce = (f32[128]{0:T(128)}, f32[128]{0:T(128)}) all-reduce(f32[128]{0:T(128)S(1)} %bitcast_reduce_fusion, f32[128]{0:T(128)S(1)} %bitcast_reduce_fusion.1), channel_id=1, replica_groups=mesh['dp'=2,'tp'=4,'cp'=4] {'tp','cp'}, use_global_device_ids=true, to_apply=%region_29.30 | all-reduce | flops 256 | bytes 2048 | tf_op jit(solution)/shard_map/psum | solution.py:149
  1140.1 361.0 %all-reduce.9.cloned.1.call-done = f32[1,1024,3072]{2,1,0:T(8,128)} async-done(((f32[1,1024,3072]{2,1,0:T(8,128)}), f32[1,1024,3072]{2,1,0:T(8,128)}) %all-reduce.9.cloned.1.call-update) | async-done | bytes 12582928 | tf_op jit(solution)/shard_map/psum | solution.py:148
  1509.3 12.6 all-reduce.1
  1522.0 13.1 fusion.81
  1535.1 391.7 %all-reduce.11.cloned.1.call-done = (f32[3072,768]{1,0:T(8,128)}, f32[3072,256]{1,0:T(8,128)}, f32[3072,256]{1,0:T(8,128)}, f32[768,3072]{1,0:T(8,128)}) async-done(((f32[3072,768]{1,0:T(8,128)}, f32[3072,256]{1,0:T(8,128)}, f32[3072,256]{1,0:T(8,128)}, f32[768,3072]{1,0:T(8,128)}), (f32[3072,768]{1,0:T(8,128)}, f32[3072,256]{1,0:T(8,128)}, f32[3072,256]{1,0:T(8,128)}, ...) | async-done | bytes 25165840 | tf_op jit(solution)/shard_map/psum | solution.py:145
  1926.7 9.3 copy.240
  (318 shorter events, 213.5 us)
Async XLA Ops:
  7.2 677.7 %all-reduce.7.cloned.1.call-start = ((), (), s32[]{:S(2)}) async-start(), calls=%async_computation | async-start | bytes 25165824 | tf_op jit(solution)/shard_map/psum | solution.py:116
  25.6 21.6 %copy-start.23 = (f32[1024,64]{0,1:T(8,128)}, f32[1024,64]{0,1:T(8,128)S(1)}, u32[]{:S(2)}) copy-start(f32[1024,64]{0,1:T(8,128)S(1)} %get-tuple-element.294) | copy-start | bytes 786436
  50.7 15.9 copy-start.5
  78.2 13.6 copy-start.6
  78.2 13.6 copy-start.7
  92.7 10.1 collective-permute-start
  93.3 8.9 collective-permute-start.2
  95.9 31.9 %collective-permute-start.1 = (bf16[1,1024,2,128]{3,1,2,0:T(8,128)(2,1)}, bf16[1,1024,2,128]{3,1,2,0:T(8,128)(2,1)}, u32[]{:S(2)}, u32[]{:S(2)}) collective-permute-start(bf16[1,1024,2,128]{3,1,2,0:T(8,128)(2,1)} %get-tuple-element.450), channel_id=1, source_target_pairs={{0,1},{1,2},{2,3},{3,0},{4,5},{5,6},{6,7},{7,4},{8,9},{9,10},{10,1... | collective-permute-start | bytes 1572872 | tf_op jit(solution)/shard_map/while/body/eval_jaxpr/ppermute | solution.py:107
  143.7 9.3 collective-permute-start
  143.7 8.6 collective-permute-start.2
  146.2 31.9 %collective-permute-start.1 = (bf16[1,1024,2,128]{3,1,2,0:T(8,128)(2,1)}, bf16[1,1024,2,128]{3,1,2,0:T(8,128)(2,1)}, u32[]{:S(2)}, u32[]{:S(2)}) collective-permute-start(bf16[1,1024,2,128]{3,1,2,0:T(8,128)(2,1)} %get-tuple-element.450), channel_id=1, source_target_pairs={{0,1},{1,2},{2,3},{3,0},{4,5},{5,6},{6,7},{7,4},{8,9},{9,10},{10,1... | collective-permute-start | bytes 1572872 | tf_op jit(solution)/shard_map/while/body/eval_jaxpr/ppermute | solution.py:107
  194.0 9.3 collective-permute-start
  194.0 8.6 collective-permute-start.2
  196.4 31.9 %collective-permute-start.1 = (bf16[1,1024,2,128]{3,1,2,0:T(8,128)(2,1)}, bf16[1,1024,2,128]{3,1,2,0:T(8,128)(2,1)}, u32[]{:S(2)}, u32[]{:S(2)}) collective-permute-start(bf16[1,1024,2,128]{3,1,2,0:T(8,128)(2,1)} %get-tuple-element.450), channel_id=1, source_target_pairs={{0,1},{1,2},{2,3},{3,0},{4,5},{5,6},{6,7},{7,4},{8,9},{9,10},{10,1... | collective-permute-start | bytes 1572872 | tf_op jit(solution)/shard_map/while/body/eval_jaxpr/ppermute | solution.py:107
  244.2 470.1 %copy-start.31 = (f32[1,2,3,1024]{3,2,1,0:T(4,128)}, f32[1,2,3,1024]{3,2,1,0:T(4,128)S(1)}, u32[]{:S(2)}) copy-start(f32[1,2,3,1024]{3,2,1,0:T(4,128)S(1)} %get-tuple-element.124) | copy-start | bytes 73732
  258.4 1242.8 %all-reduce.9.cloned.1.call-start = ((), (), s32[]{:S(2)}) async-start(), calls=%async_computation.1 | async-start | bytes 25165824 | tf_op jit(solution)/shard_map/psum | solution.py:148
  684.8 15.6 slice-start
  684.8 15.6 slice-start.2
  690.5 23.8 %slice-start.9 = ((s8[4718592]{0:T(1024)(128)(4,1)}), s8[4194304]{0:T(1024)(128)(4,1)S(1)}, s32[]{:S(2)}) async-start(s8[4718592]{0:T(1024)(128)(4,1)} %bitcast.493), calls=%async_computation.12 | async-start | bytes 8388608
  700.5 13.8 copy-start.26
  700.5 13.8 slice-start.10
  785.5 10.4 collective-permute-start.3
  785.6 8.6 collective-permute-start.5
  787.2 21.5 %collective-permute-start.4 = (bf16[1,1024,2,128]{3,1,2,0:T(8,128)(2,1)}, bf16[1,1024,2,128]{3,1,2,0:T(8,128)(2,1)}, u32[]{:S(2)}, u32[]{:S(2)}) collective-permute-start(bf16[1,1024,2,128]{3,1,2,0:T(8,128)(2,1)} %get-tuple-element.483), channel_id=1, source_target_pairs={{0,1},{1,2},{2,3},{3,0},{4,5},{5,6},{6,7},{7,4},{8,9},{9,10},{10,1... | collective-permute-start | bytes 1572872 | tf_op jit(solution)/shard_map/while/body/eval_jaxpr/ppermute | solution.py:132
  787.2 53.2 %collective-permute-start.6 = (f32[1,1024,2,128]{3,1,2,0:T(8,128)}, f32[1,1024,2,128]{3,1,2,0:T(8,128)}, u32[]{:S(2)}, u32[]{:S(2)}) collective-permute-start(f32[1,1024,2,128]{3,1,2,0:T(8,128)} %get-tuple-element.485), channel_id=1, source_target_pairs={{0,1},{1,2},{2,3},{3,0},{4,5},{5,6},{6,7},{7,4},{8,9},{9,10},{10,1... | collective-permute-start | bytes 3145736 | tf_op jit(solution)/shard_map/while/body/eval_jaxpr/ppermute | solution.py:132
  787.9 62.0 %collective-permute-start.7 = (f32[1,1024,2,128]{3,1,2,0:T(8,128)}, f32[1,1024,2,128]{3,1,2,0:T(8,128)}, u32[]{:S(2)}, u32[]{:S(2)}) collective-permute-start(f32[1,1024,2,128]{3,1,2,0:T(8,128)} %get-tuple-element.486), channel_id=1, source_target_pairs={{0,1},{1,2},{2,3},{3,0},{4,5},{5,6},{6,7},{7,4},{8,9},{9,10},{10,1... | collective-permute-start | bytes 3145736 | tf_op jit(solution)/shard_map/while/body/eval_jaxpr/ppermute | solution.py:132
  862.0 10.3 collective-permute-start.3
  862.0 8.6 collective-permute-start.5
  863.6 21.5 %collective-permute-start.4 = (bf16[1,1024,2,128]{3,1,2,0:T(8,128)(2,1)}, bf16[1,1024,2,128]{3,1,2,0:T(8,128)(2,1)}, u32[]{:S(2)}, u32[]{:S(2)}) collective-permute-start(bf16[1,1024,2,128]{3,1,2,0:T(8,128)(2,1)} %get-tuple-element.483), channel_id=1, source_target_pairs={{0,1},{1,2},{2,3},{3,0},{4,5},{5,6},{6,7},{7,4},{8,9},{9,10},{10,1... | collective-permute-start | bytes 1572872 | tf_op jit(solution)/shard_map/while/body/eval_jaxpr/ppermute | solution.py:132
  863.6 53.3 %collective-permute-start.6 = (f32[1,1024,2,128]{3,1,2,0:T(8,128)}, f32[1,1024,2,128]{3,1,2,0:T(8,128)}, u32[]{:S(2)}, u32[]{:S(2)}) collective-permute-start(f32[1,1024,2,128]{3,1,2,0:T(8,128)} %get-tuple-element.485), channel_id=1, source_target_pairs={{0,1},{1,2},{2,3},{3,0},{4,5},{5,6},{6,7},{7,4},{8,9},{9,10},{10,1... | collective-permute-start | bytes 3145736 | tf_op jit(solution)/shard_map/while/body/eval_jaxpr/ppermute | solution.py:132
  864.2 62.0 %collective-permute-start.7 = (f32[1,1024,2,128]{3,1,2,0:T(8,128)}, f32[1,1024,2,128]{3,1,2,0:T(8,128)}, u32[]{:S(2)}, u32[]{:S(2)}) collective-permute-start(f32[1,1024,2,128]{3,1,2,0:T(8,128)} %get-tuple-element.486), channel_id=1, source_target_pairs={{0,1},{1,2},{2,3},{3,0},{4,5},{5,6},{6,7},{7,4},{8,9},{9,10},{10,1... | collective-permute-start | bytes 3145736 | tf_op jit(solution)/shard_map/while/body/eval_jaxpr/ppermute | solution.py:132
  938.4 10.3 collective-permute-start.3
  938.4 8.6 collective-permute-start.5
  940.0 21.5 %collective-permute-start.4 = (bf16[1,1024,2,128]{3,1,2,0:T(8,128)(2,1)}, bf16[1,1024,2,128]{3,1,2,0:T(8,128)(2,1)}, u32[]{:S(2)}, u32[]{:S(2)}) collective-permute-start(bf16[1,1024,2,128]{3,1,2,0:T(8,128)(2,1)} %get-tuple-element.483), channel_id=1, source_target_pairs={{0,1},{1,2},{2,3},{3,0},{4,5},{5,6},{6,7},{7,4},{8,9},{9,10},{10,1... | collective-permute-start | bytes 1572872 | tf_op jit(solution)/shard_map/while/body/eval_jaxpr/ppermute | solution.py:132
  940.0 53.3 %collective-permute-start.6 = (f32[1,1024,2,128]{3,1,2,0:T(8,128)}, f32[1,1024,2,128]{3,1,2,0:T(8,128)}, u32[]{:S(2)}, u32[]{:S(2)}) collective-permute-start(f32[1,1024,2,128]{3,1,2,0:T(8,128)} %get-tuple-element.485), channel_id=1, source_target_pairs={{0,1},{1,2},{2,3},{3,0},{4,5},{5,6},{6,7},{7,4},{8,9},{9,10},{10,1... | collective-permute-start | bytes 3145736 | tf_op jit(solution)/shard_map/while/body/eval_jaxpr/ppermute | solution.py:132
  940.6 62.0 %collective-permute-start.7 = (f32[1,1024,2,128]{3,1,2,0:T(8,128)}, f32[1,1024,2,128]{3,1,2,0:T(8,128)}, u32[]{:S(2)}, u32[]{:S(2)}) collective-permute-start(f32[1,1024,2,128]{3,1,2,0:T(8,128)} %get-tuple-element.486), channel_id=1, source_target_pairs={{0,1},{1,2},{2,3},{3,0},{4,5},{5,6},{6,7},{7,4},{8,9},{9,10},{10,1... | collective-permute-start | bytes 3145736 | tf_op jit(solution)/shard_map/while/body/eval_jaxpr/ppermute | solution.py:132
  1031.9 17.4 collective-permute-start.8
  1032.9 30.5 %collective-permute-start.9 = (bf16[1,1024,2,128]{1,3,2,0:T(8,128)(2,1)}, bf16[1,1024,2,128]{1,3,2,0:T(8,128)(2,1)}, u32[]{:S(2)}, u32[]{:S(2)}) collective-permute-start(bf16[1,1024,2,128]{1,3,2,0:T(8,128)(2,1)} %copy.151), channel_id=1, source_target_pairs={{0,1},{1,2},{2,3},{3,0},{4,5},{5,6},{6,7},{7,4},{8,9},{9,10},{10,1... | collective-permute-start | bytes 1572872 | tf_op jit(solution)/shard_map/ppermute | solution.py:137
  1038.3 13.1 copy-start.9
  1038.3 13.1 copy-start.46
  1038.3 13.1 copy-start.57
  1078.2 848.5 %all-reduce.11.cloned.1.call-start = ((), (), s32[]{:S(2)}) async-start(), calls=%async_computation.2 | async-start | bytes 50331648 | tf_op jit(solution)/shard_map/psum | solution.py:145
  1078.9 20.9 %slice-start.7 = ((s8[6291456]{0:T(1024)(128)(4,1)}), s8[4194304]{0:T(1024)(128)(4,1)S(1)}, s32[]{:S(2)}) async-start(s8[6291456]{0:T(1024)(128)(4,1)} %bitcast.475), calls=%async_computation.10 | async-start | bytes 8388608
  1108.2 393.0 %copy-start.44 = (f32[3072]{0:T(1024)S(1)}, f32[3072]{0:T(1024)}, u32[]{:S(2)}) copy-start(f32[3072]{0:T(1024)} %copy-done.43) | copy-start | bytes 36868
  1108.2 393.0 %copy-start.48 = (f32[1024]{0:T(1024)S(1)}, f32[1024]{0:T(1024)}, u32[]{:S(2)}) copy-start(f32[1024]{0:T(1024)} %copy-done.47) | copy-start | bytes 12292
  1140.1 369.2 %copy-start.49 = (f32[3072]{0:T(1024)S(1)}, f32[3072]{0:T(1024)}, u32[]{:S(2)}) copy-start(f32[3072]{0:T(1024)} %get-tuple-element.213) | copy-start | bytes 36868
  1926.7 14.1 slice-start.4
  1926.7 14.1 slice-start.5
  (57 other events, 390.6 us)
Sparse Core Ops, SparseCore 0:
  258.6 426.2 all-reduce.6
  1078.3 422.8 all-reduce.8
  1504.5 422.1 all-reduce.10
where the time goes:
time: 1960 us; the launch traced here: 1950 us
  waiting for transfers between devices  1220 us (62%)
  matrix products  437 us (22%)
  other arithmetic  136 us (7%)
  local copies, waits for them, and re-layouts  86.4 us (4%)
  blocking collectives  44.5 us (2%)
    psum x1, waiting for transfers between devices, per_device(): lax.psum(jnp.einsum('bkgqd,kgdm->bqm', out_bf, wo_split, preferred_elemen...  425 us
    psum x1, waiting for transfers between devices, per_device(): lax.psum(jnp.einsum('bsd,bsh->dh', normed, dq_bf, preferred_element_type=...  392 us
    psum x1, waiting for transfers between devices, per_device(): lax.psum(jnp.einsum('bsh,dh->bsd', dq_bf, w_q, preferred_element_type=jnp...  361 us
    dot_general x4, matrix products, grad_block(): jnp.einsum('bkgqd,bskd->bkgqs', d_out, v_blk, preferred_element_type=jnp....  69.9 us
    dot_general x4, matrix products, attend_block(): jnp.einsum('bkgqs,bskd->bkgqd', attn_prob.astype(jnp.bfloat16), v_blk, pr...  55.8 us
    dot_general x4, matrix products, grad_block(): jnp.einsum('bkgqs,bkgqd->bskd', attn_prob.astype(jnp.bfloat16), d_out, pr...  48.9 us
    dot_general x4, matrix products, attend_block(): jnp.einsum('bqkgd,bskd->bkgqs', q_fin, k_blk, preferred_element_type=jnp....  47.9 us
    reduce_sum x4, other arithmetic, attend_block(): new_sum = run_sum * factor + jnp.sum(attn_prob, axis=-1)  45.7 us
  transfers between devices with their start and end apart: 29, of which 9 were waited for; matrix products, arithmetic and copies ran while one was open for 17% of the time, Pallas kernels for 0%

commit v1 on v0

v1 whole, which is shorter than its diff:
```python
import functools

import jax
import jax.numpy as jnp
import numpy as np
from jax import lax
from jax.experimental import pallas as pl
from jax.experimental.pallas import tpu as pltpu
from jax.sharding import PartitionSpec as P

EPS = 1e-6
ROPE_BASE = 1000000.0
ROPE_SCALE = 8.0
NEG_BIG = -1e30
LOG2E = 1.4426950408889634
HD = 128
F32 = jnp.float32
BF16 = jnp.bfloat16
VMEM_MAX = 60 * 1024 * 1024
NT = (((1,), (1,)), ((), ()))
TN = (((0,), (0,)), ((), ()))


def dot(a, b, dims=(((1,), (0,)), ((), ()))):
    return lax.dot_general(a, b, dims, preferred_element_type=F32)


def params(sem, vmem=VMEM_MAX):
    return pltpu.CompilerParams(dimension_semantics=sem, vmem_limit_bytes=vmem)


def cost(flops, nbytes, trans=0):
    return pl.CostEstimate(flops=int(flops), bytes_accessed=int(nbytes), transcendentals=int(trans))


def whole(shape):
    return pl.BlockSpec(shape, lambda *_: (0,) * len(shape))


def fixed(shape):
    return pl.BlockSpec(shape, lambda *_: (0,) * len(shape), pipeline_mode=pl.Buffered(buffer_count=1))


def rope_tables(pos_loc):
    half_dim = HD // 2
    inv_freq = 1.0 / (ROPE_SCALE * ROPE_BASE ** (jnp.arange(half_dim, dtype=F32) * (2.0 / HD)))
    angles = pos_loc.astype(F32)[:, None] * inv_freq[None, :]
    cos_t, sin_t = jnp.cos(angles), jnp.sin(angles)
    return jnp.concatenate([cos_t, cos_t], axis=-1), jnp.concatenate([-sin_t, sin_t], axis=-1)


def norm_rope(raw, gain, cos_t, sin_t):
    raw = raw.astype(F32)
    unit = raw * lax.rsqrt(jnp.mean(raw * raw, axis=-1, keepdims=True) + EPS)
    scaled = unit * (1.0 + gain)
    return (scaled * cos_t + pltpu.roll(scaled, HD // 2, 1) * sin_t).astype(BF16)


def norm_rope_back(d_final, raw, gain, cos_t, sin_t):
    raw = raw.astype(F32)
    inv = lax.rsqrt(jnp.mean(raw * raw, axis=-1, keepdims=True) + EPS)
    unit = raw * inv
    d_scaled = d_final * cos_t - pltpu.roll(d_final, HD // 2, 1) * sin_t
    d_gain = jnp.sum(d_scaled * unit, axis=0, keepdims=True)
    d_unit = d_scaled * (1.0 + gain)
    d_raw = inv * (d_unit - unit * jnp.mean(d_unit * unit, axis=-1, keepdims=True))
    return d_raw.astype(BF16), d_gain


def kv_kernel(x_ref, wpre_ref, wk_ref, wv_ref, kn_ref, cos_ref, sin_ref, normed_ref, kv_ref, kraw_ref):
    x = x_ref[...].astype(F32)
    inv = lax.rsqrt(jnp.mean(x * x, axis=-1, keepdims=True) + EPS)
    normed = (x * inv * (1.0 + wpre_ref[...])).astype(BF16)
    normed_ref[...] = normed
    k_raw = dot(normed, wk_ref[...]).astype(BF16)
    kraw_ref[...] = k_raw
    width = k_raw.shape[1]
    for h in range(width // HD):
        cols = slice(h * HD, (h + 1) * HD)
        kv_ref[:, cols] = norm_rope(k_raw[:, cols], kn_ref[...], cos_ref[...], sin_ref[...])
    kv_ref[:, width:] = dot(normed, wv_ref[...]).astype(BF16)


def project_kv(x, w_pre, w_k, w_v, k_norm, cos_t, sin_t, rows=256):
    seq, dim = x.shape
    width = w_k.shape[1]
    row = lambda n: pl.BlockSpec((rows, n), lambda i: (i, 0))
    return pl.pallas_call(
        kv_kernel,
        name="project_kv",
        grid=(seq // rows,),
        in_specs=[row(dim), whole((1, dim)), fixed(w_k.shape), fixed(w_v.shape), whole((1, HD)), row(HD), row(HD)],
        out_specs=[row(dim), row(2 * width), row(width)],
        out_shape=[
            jax.ShapeDtypeStruct((seq, dim), BF16),
            jax.ShapeDtypeStruct((seq, 2 * width), BF16),
            jax.ShapeDtypeStruct((seq, width), BF16),
        ],
        compiler_params=params(("arbitrary",)),
        cost_estimate=cost(4 * seq * dim * width, 4 * seq * dim + 4 * dim * width),
    )(x, w_pre, w_k, w_v, k_norm, cos_t, sin_t)


def q_kernel(normed_ref, wq_ref, qn_ref, cos_ref, sin_ref, qfin_ref, qraw_ref):
    q_raw = dot(normed_ref[...], wq_ref[...]).astype(BF16)
    for h in range(qfin_ref.shape[0]):
        part = q_raw[:, h * HD:(h + 1) * HD]
        qraw_ref[h] = part
        qfin_ref[h] = norm_rope(part, qn_ref[...], cos_ref[...], sin_ref[...])


def project_q(normed, w_q, q_norm, cos_t, sin_t, rows=256):
    seq, dim = normed.shape
    heads = w_q.shape[1] // HD
    row = lambda n: pl.BlockSpec((rows, n), lambda i: (i, 0))
    head_rows = pl.BlockSpec((heads, rows, HD), lambda i: (0, i, 0))
    shape = jax.ShapeDtypeStruct((heads, seq, HD), BF16)
    return pl.pallas_call(
        q_kernel,
        name="project_q",
        grid=(seq // rows,),
        in_specs=[row(dim), fixed(w_q.shape), whole((1, HD)), row(HD), row(HD)],
        out_specs=[head_rows, head_rows],
        out_shape=[shape, shape],
        compiler_params=params(("arbitrary",)),
        cost_estimate=cost(2 * seq * dim * heads * HD, 2 * seq * dim + 2 * dim * heads * HD),
    )(normed, w_q, q_norm, cos_t, sin_t)


def load_kv(kv_refs, k_buf, v_buf, sems):
    kv_heads = k_buf.shape[0]
    copies = []
    for s, ref in enumerate(kv_refs):
        for h in range(kv_heads):
            for t, buf in enumerate((k_buf, v_buf)):
                src = ref.at[:, pl.ds((t * kv_heads + h) * HD, HD)]
                copies.append(pltpu.make_async_copy(src, buf.at[h, s], sems.at[s, h, t]))
    for copy in copies:
        copy.start()
    for copy in copies:
        copy.wait()


def piece_place(piece, me, n_cp):
    upper = piece >= n_cp
    owner = jnp.where(upper, 2 * n_cp - 1 - piece, piece)
    return jnp.bitwise_xor(owner, me), upper.astype(jnp.int32)


def fwd_kernel(n_cp, me_ref, q_ref, *rest):
    kv_refs = rest[:n_cp]
    o_ref, lse_ref, k_buf, v_buf, m_scr, acc_scr, sems = rest[n_cp:]
    h, half = pl.program_id(0), pl.program_id(1)
    groups, rows, _ = q_ref.shape

    @pl.when((h == 0) & (half == 0))
    def _():
        load_kv(kv_refs, k_buf, v_buf, sems)

    me = me_ref[0]
    piece = jnp.where(half == 0, me, 2 * n_cp - 1 - me)
    scale = HD ** -0.5 * LOG2E
    m_scr[...] = jnp.full(m_scr.shape, NEG_BIG, F32)
    acc_scr[...] = jnp.zeros(acc_scr.shape, F32)

    def block(j, masked):
        slot, upper = piece_place(j, me, n_cp)
        span = pl.ds(pl.multiple_of(upper * rows, rows), rows)
        k = k_buf[h, slot, span, :]
        v_ext = jnp.concatenate([v_buf[h, slot, span, :], jnp.ones((rows, HD), BF16)], axis=1)
        scores = [dot(q_ref[g], k, NT) * scale for g in range(groups)]
        for g in range(groups):
            s = scores[g]
            if masked:
                q_pos = lax.broadcasted_iota(jnp.int32, s.shape, 0)
                k_pos = lax.broadcasted_iota(jnp.int32, s.shape, 1)
                s = jnp.where(k_pos <= q_pos, s, NEG_BIG)
            m_old = m_scr[g]
            m_new = jnp.maximum(m_old, jnp.max(s, axis=1, keepdims=True))
            alpha = jnp.exp2(m_old - m_new)
            p = jnp.exp2(s - jnp.concatenate([m_new] * (rows // HD), axis=1)).astype(BF16)
            acc_scr[g] = acc_scr[g] * jnp.concatenate([alpha, alpha], axis=1) + dot(p, v_ext)
            m_scr[g] = m_new

    def full(j, carry):
        block(j, False)
        return carry

    lax.fori_loop(0, piece, full, 0)
    block(piece, True)
    for g in range(groups):
        l = acc_scr[g, :, HD:]
        o_ref[:, g * HD:(g + 1) * HD] = (acc_scr[g, :, :HD] / l).astype(BF16)
        lse_ref[0, g:g + 1, :] = jnp.transpose(m_scr[g] + jnp.log2(l))[0:1, :]


def attention_fwd(me, q_fin, kv_blocks, kv_heads):
    heads, seq, _ = q_fin.shape
    n_cp = len(kv_blocks)
    groups = heads // kv_heads
    rows = seq // 2
    grid_spec = pltpu.PrefetchScalarGridSpec(
        num_scalar_prefetch=1,
        grid=(kv_heads, 2),
        in_specs=[pl.BlockSpec((groups, rows, HD), lambda h, i, *_: (h, i, 0))] + [pl.BlockSpec(memory_space=pl.ANY)] * n_cp,
        out_specs=[
            pl.BlockSpec((rows, groups * HD), lambda h, i, *_: (i, h)),
            pl.BlockSpec((1, 8, rows), lambda h, i, *_: (h, 0, i)),
        ],
        scratch_shapes=[
            pltpu.VMEM((kv_heads, n_cp, seq, HD), BF16),
            pltpu.VMEM((kv_heads, n_cp, seq, HD), BF16),
            pltpu.VMEM((groups, rows, HD), F32),
            pltpu.VMEM((groups, rows, 2 * HD), F32),
            pltpu.SemaphoreType.DMA((n_cp, kv_heads, 2)),
        ],
    )
    pairs = heads * rows * rows * (2 * n_cp + 1)
    return pl.pallas_call(
        functools.partial(fwd_kernel, n_cp),
        name="attention_fwd",
        grid_spec=grid_spec,
        out_shape=[
            jax.ShapeDtypeStruct((seq, heads * HD), BF16),
            jax.ShapeDtypeStruct((kv_heads, 8, seq), F32),
        ],
        compiler_params=params(("arbitrary", "arbitrary")),
        cost_estimate=cost(4 * pairs * HD, 8 * seq * heads * HD, pairs),
    )(me, q_fin, *kv_blocks)


def bwd_kernel(n_cp, me_ref, q_ref, do_ref, o_ref, lse_ref, qraw_ref, cos_ref, sin_ref, qn_ref, *rest):
    kv_refs = rest[:n_cp]
    dq_ref, dkv_ref, gain_ref, k_buf, v_buf, dq_scr, sems = rest[n_cp:]
    h, half = pl.program_id(0), pl.program_id(1)
    groups, rows, _ = q_ref.shape

    @pl.when((h == 0) & (half == 0))
    def _():
        load_kv(kv_refs, k_buf, v_buf, sems)
        gain_ref[...] = jnp.zeros(gain_ref.shape, F32)

    @pl.when(half == 0)
    def _():
        dkv_ref[...] = jnp.zeros(dkv_ref.shape, F32)

    me = me_ref[0]
    piece = jnp.where(half == 0, me, 2 * n_cp - 1 - me)
    scale = HD ** -0.5
    delta = []
    for g in range(groups):
        prod = do_ref[g].astype(F32) * o_ref[:, g * HD:(g + 1) * HD].astype(F32)
        column = jnp.broadcast_to(jnp.sum(prod, axis=1, keepdims=True), (rows, HD))
        delta.append(jnp.transpose(column)[0:1, :])
    dq_scr[...] = jnp.zeros(dq_scr.shape, F32)

    def block(j, masked):
        slot, upper = piece_place(j, me, n_cp)
        span = pl.ds(pl.multiple_of(upper * rows, rows), rows)
        k = k_buf[h, slot, span, :]
        v = v_buf[h, slot, span, :]
        probs, d_scores = [], []
        for g in range(groups):
            s = dot(k, q_ref[g], NT)
            p = jnp.exp2(s * (scale * LOG2E) - lse_ref[0, g:g + 1, :])
            if masked:
                k_pos = lax.broadcasted_iota(jnp.int32, s.shape, 0)
                q_pos = lax.broadcasted_iota(jnp.int32, s.shape, 1)
                p = jnp.where(k_pos <= q_pos, p, 0.0)
            probs.append(p.astype(BF16))
            d_scores.append((p * (dot(v, do_ref[g], NT) - delta[g])).astype(BF16))
        for g in range(groups):
            dq_scr[g] += dot(d_scores[g], k, TN)
        index = (slot % 2) * (n_cp // 2) + slot // 2
        d_all = jnp.concatenate(d_scores, axis=1)
        p_all = jnp.concatenate(probs, axis=1)
        dkv_ref[index, 0, 0, span, :] += dot(d_all, q_ref[...].reshape(groups * rows, HD)) * scale
        dkv_ref[index, 1, 0, span, :] += dot(p_all, do_ref[...].reshape(groups * rows, HD))

    def full(j, carry):
        block(j, False)
        return carry

    lax.fori_loop(0, piece, full, 0)
    block(piece, True)
    for g in range(groups):
        d_raw, d_gain = norm_rope_back(dq_scr[g] * scale, qraw_ref[g], qn_ref[...], cos_ref[...], sin_ref[...])
        dq_ref[:, g * HD:(g + 1) * HD] = d_raw
        gain_ref[0:1, :] += d_gain


def attention_bwd(me, q_fin, d_out, out, lse, q_raw, cos_t, sin_t, q_norm, kv_blocks, kv_heads):
    heads, seq, _ = q_fin.shape
    n_cp = len(kv_blocks)
    groups = heads // kv_heads
    rows = seq // 2
    by_head = pl.BlockSpec((groups, rows, HD), lambda h, i, *_: (h, i, 0))
    by_row = pl.BlockSpec((rows, groups * HD), lambda h, i, *_: (i, h))
    table = pl.BlockSpec((rows, HD), lambda h, i, *_: (i, 0))
    grid_spec = pltpu.PrefetchScalarGridSpec(
        num_scalar_prefetch=1,
        grid=(kv_heads, 2),
        in_specs=[
            by_head,
            by_head,
            by_row,
            pl.BlockSpec((1, 8, rows), lambda h, i, *_: (h, 0, i)),
            by_head,
            table,
            table,
            whole((1, HD)),
        ] + [pl.BlockSpec(memory_space=pl.ANY)] * n_cp,
        out_specs=[
            by_row,
            pl.BlockSpec((n_cp, 2, 1, seq, HD), lambda h, i, *_: (0, 0, h, 0, 0)),
            whole((8, HD)),
        ],
        scratch_shapes=[
            pltpu.VMEM((kv_heads, n_cp, seq, HD), BF16),
            pltpu.VMEM((kv_heads, n_cp, seq, HD), BF16),
            pltpu.VMEM((groups, rows, HD), F32),
            pltpu.SemaphoreType.DMA((n_cp, kv_heads, 2)),
        ],
    )
    pairs = heads * rows * rows * (2 * n_cp + 1)
    return pl.pallas_call(
        functools.partial(bwd_kernel, n_cp),
        name="attention_bwd",
        grid_spec=grid_spec,
        out_shape=[
            jax.ShapeDtypeStruct((seq, heads * HD), BF16),
            jax.ShapeDtypeStruct((n_cp, 2, kv_heads, seq, HD), F32),
            jax.ShapeDtypeStruct((8, HD), F32),
        ],
        compiler_params=params(("arbitrary", "arbitrary")),
        cost_estimate=cost(10 * pairs * HD, 16 * seq * heads * HD, pairs),
    )(me, q_fin, d_out, out, lse, q_raw, cos_t, sin_t, q_norm, *kv_blocks)


def post_kernel(o_ref, wall_ref, wmine_ref, x_ref, dy_ref, wpost_ref, y_ref, dattn_ref, do_ref, dpost_ref):
    n_tp = o_ref.shape[0]
    out_all = jnp.concatenate([o_ref[t] for t in range(n_tp)], axis=1)
    attn = dot(out_all, wall_ref[...])
    inv = lax.rsqrt(jnp.mean(attn * attn, axis=-1, keepdims=True) + EPS)
    unit = attn * inv
    gain = 1.0 + wpost_ref[...]
    y_ref[...] = (x_ref[...].astype(F32) + unit * gain).astype(BF16)
    dy = dy_ref[...].astype(F32)

    @pl.when(pl.program_id(0) == 0)
    def _():
        dpost_ref[...] = jnp.zeros(dpost_ref.shape, F32)

    dpost_ref[0:1, :] += jnp.sum(dy * unit, axis=0, keepdims=True)
    d_unit = dy * gain
    d_attn = (inv * (d_unit - unit * jnp.mean(d_unit * unit, axis=-1, keepdims=True))).astype(BF16)
    dattn_ref[...] = d_attn
    d_out = dot(d_attn, wmine_ref[...], NT)
    for h in range(do_ref.shape[0]):
        do_ref[h] = d_out[:, h * HD:(h + 1) * HD].astype(BF16)


def post(out_all, w_all, w_mine, x, dy, w_post, rows=256):
    n_tp, seq, width = out_all.shape
    dim = x.shape[1]
    heads = width // HD
    row = pl.BlockSpec((rows, dim), lambda i: (i, 0))
    return pl.pallas_call(
        post_kernel,
        name="post",
        grid=(seq // rows,),
        in_specs=[
            pl.BlockSpec((n_tp, rows, width), lambda i: (0, i, 0)),
            fixed(w_all.shape),
            fixed(w_mine.shape),
            row,
            row,
            whole((1, dim)),
        ],
        out_specs=[row, row, pl.BlockSpec((heads, rows, HD), lambda i: (0, i, 0)), whole((8, dim))],
        out_shape=[
            jax.ShapeDtypeStruct((seq, dim), BF16),
            jax.ShapeDtypeStruct((seq, dim), BF16),
            jax.ShapeDtypeStruct((heads, seq, HD), BF16),
            jax.ShapeDtypeStruct((8, dim), F32),
        ],
        compiler_params=params(("arbitrary",)),
        cost_estimate=cost(2 * seq * dim * width * (n_tp + 1), 8 * seq * dim + 2 * dim * width * (n_tp + 1)),
    )(out_all, w_all, w_mine, x, dy, w_post)


def kback_kernel(own_ref, near_ref, far_ref, kraw_ref, cos_ref, sin_ref, kn_ref, out_ref, gain_ref):
    @pl.when(pl.program_id(0) == 0)
    def _():
        gain_ref[...] = jnp.zeros(gain_ref.shape, F32)

    kv_heads = own_ref.shape[2]
    for h in range(kv_heads):
        cols = slice(h * HD, (h + 1) * HD)
        d_k = own_ref[0, 0, h] + near_ref[0, 0, h] + far_ref[0, h]
        d_raw, d_gain = norm_rope_back(d_k, kraw_ref[:, cols], kn_ref[...], cos_ref[...], sin_ref[...])
        out_ref[:, cols] = d_raw
        gain_ref[0:1, :] += d_gain
        d_v = own_ref[0, 1, h] + near_ref[0, 1, h] + far_ref[1, h]
        out_ref[:, (kv_heads + h) * HD:(kv_heads + h + 1) * HD] = d_v.astype(BF16)


def key_back(dkv, near, far, k_raw, cos_t, sin_t, k_norm, rows=256):
    _, _, kv_heads, seq, _ = dkv.shape
    full = pl.BlockSpec((1, 2, kv_heads, rows, HD), lambda i: (0, 0, 0, i, 0))
    row = lambda n: pl.BlockSpec((rows, n), lambda i: (i, 0))
    return pl.pallas_call(
        kback_kernel,
        name="key_back",
        grid=(seq // rows,),
        in_specs=[
            full,
            full,
            pl.BlockSpec((2, kv_heads, rows, HD), lambda i: (0, 0, i, 0)),
            row(kv_heads * HD),
            row(HD),
            row(HD),
            whole((1, HD)),
        ],
        out_specs=[row(2 * kv_heads * HD), whole((8, HD))],
        out_shape=[
            jax.ShapeDtypeStruct((seq, 2 * kv_heads * HD), BF16),
            jax.ShapeDtypeStruct((8, HD), F32),
        ],
        compiler_params=params(("arbitrary",)),
        cost_estimate=cost(50 * seq * kv_heads * HD, 12 * seq * kv_heads * HD),
    )(dkv, near, far, k_raw, cos_t, sin_t, k_norm)


def dx_kernel(n_tp, *refs):
    g_refs = refs[:n_tp]
    w_ref, x_ref, dy_ref, wpre_ref, dx_ref, dpre_ref, acc = refs[n_tp:]
    i = pl.program_id(0)
    total = dot(g_refs[0][...], w_ref[0], NT)
    for t in range(1, n_tp):
        total += dot(g_refs[t][...], w_ref[t], NT)
    acc[i] = total

    @pl.when(i == pl.num_programs(0) - 1)
    def _():
        d_normed = jnp.concatenate([acc[t] for t in range(acc.shape[0])], axis=1)
        x = x_ref[...].astype(F32)
        inv = lax.rsqrt(jnp.mean(x * x, axis=-1, keepdims=True) + EPS)
        unit = x * inv
        dpre_ref[...] = jnp.broadcast_to(jnp.sum(d_normed * unit, axis=0, keepdims=True), dpre_ref.shape)
        d_unit = d_normed * (1.0 + wpre_ref[...])
        d_x = inv * (d_unit - unit * jnp.mean(d_unit * unit, axis=-1, keepdims=True))
        dx_ref[...] = (dy_ref[...].astype(F32) + d_x).astype(BF16)


def input_grad(grads, w_all, x, dy, w_pre, cols=512):
    n_tp = len(grads)
    rows, width = grads[0].shape
    dim = x.shape[1]
    return pl.pallas_call(
        functools.partial(dx_kernel, n_tp),
        name="input_grad",
        grid=(dim // cols,),
        in_specs=[whole((rows, width))] * n_tp + [
            pl.BlockSpec((n_tp, cols, width), lambda i: (0, i, 0)),
            whole((rows, dim)),
            whole((rows, dim)),
            whole((1, dim)),
        ],
        out_specs=[whole((rows, dim)), whole((8, dim))],
        out_shape=[jax.ShapeDtypeStruct((rows, dim), BF16), jax.ShapeDtypeStruct((8, dim), F32)],
        scratch_shapes=[pltpu.VMEM((dim // cols, rows, cols), F32)],
        compiler_params=params(("arbitrary",)),
        cost_estimate=cost(2 * n_tp * rows * width * dim, 2 * n_tp * width * dim),
    )(*grads, w_all, x, dy, w_pre)


def solution(mesh):
    n_cp, n_tp, n_dp = mesh.shape["cp"], mesh.shape["tp"], mesh.shape["dp"]
    near = [(i, i ^ 1) for i in range(n_cp)]
    across = [(i, i ^ 2) for i in range(n_cp)]

    def per_device(hidden, cotangent, pos_loc, w_q, w_k, w_v, w_o, w_pre, w_post, q_norm, k_norm):
        _, seq, dim = hidden.shape
        x, dy = hidden[0], cotangent[0]
        kv_heads = w_k.shape[1] // HD
        cp, tp, dp = lax.axis_index("cp"), lax.axis_index("tp"), lax.axis_index("dp")
        me = cp.astype(jnp.int32).reshape(1)
        everyone = ("tp", "dp", "cp")
        share = dp * n_cp + cp
        shares = n_dp * n_cp

        o_rows = w_o.shape[0] // shares
        w_o_all = lax.all_gather(lax.dynamic_slice_in_dim(w_o, share * o_rows, o_rows, 0), everyone, axis=0, tiled=True)
        w_rows = dim // shares
        parts = [lax.dynamic_slice_in_dim(w, share * w_rows, w_rows, 0) for w in (w_q, w_k, w_v)]

        cos_t, sin_t = rope_tables(pos_loc)
        qn, kn = q_norm.reshape(1, HD), k_norm.reshape(1, HD)
        wpre, wpost = w_pre.reshape(1, dim), w_post.reshape(1, dim)
        normed, kv_own, k_raw = project_kv(x, wpre, w_k, w_v, kn, cos_t, sin_t)
        kv_far = lax.ppermute(kv_own, "cp", across)
        kv_near = lax.ppermute(kv_own, "cp", near)
        kv_both = lax.ppermute(kv_far, "cp", near)
        q_fin, q_raw = project_q(normed, w_q, qn, cos_t, sin_t)
        kv_blocks = [kv_own, kv_near, kv_far, kv_both]
        out, lse = attention_fwd(me, q_fin, kv_blocks, kv_heads)

        out, w_o_all = lax.optimization_barrier((out, w_o_all))
        out_all = lax.all_gather(out, "tp", axis=0, tiled=False)
        y, d_attn, d_out, d_post = post(out_all, w_o_all, w_o, x, dy, wpost)
        fence, _ = lax.optimization_barrier((jnp.concatenate(parts, axis=1), out_all))
        w_all = lax.all_gather(fence, everyone, axis=0, tiled=True).reshape(n_tp, dim, fence.shape[1])

        def cp_sum(part):
            half = part.shape[0] // 2
            core = cp % 2
            keep = lax.dynamic_slice_in_dim(part, core * half, half, 0)
            give = lax.dynamic_slice_in_dim(part, (1 - core) * half, half, 0)
            keep = keep + lax.ppermute(give, "cp", near)
            keep = keep + lax.ppermute(keep, "cp", across)
            other = lax.ppermute(keep, "cp", near)
            first = jnp.where(core == 0, keep, other)
            second = jnp.where(core == 0, other, keep)
            return jnp.concatenate([first, second], axis=0)

        d_wo_part, d_out = lax.optimization_barrier((dot(out, d_attn, TN), d_out))
        d_wo = cp_sum(d_wo_part)

        dq, dkv, dq_gain = attention_bwd(me, q_fin, d_out, out, lse, q_raw, cos_t, sin_t, qn, kv_blocks, kv_heads)
        got = lax.ppermute(dkv[n_cp // 2:], "cp", near)
        dkv_far = lax.ppermute(dkv[1] + got[1], "cp", across)
        d_kv, dk_gain = key_back(dkv, got, dkv_far, k_raw, cos_t, sin_t, kn)

        rows = seq // n_tp
        grads = jnp.concatenate([dq, d_kv], axis=1)
        pieces = [None] * n_tp
        pieces[0] = lax.dynamic_slice_in_dim(grads, tp * rows, rows, 0)
        for s in range(1, n_tp):
            part = lax.dynamic_slice_in_dim(grads, ((tp + s) % n_tp) * rows, rows, 0)
            pieces[s] = lax.ppermute(part, "tp", [(i, (i + s) % n_tp) for i in range(n_tp)])
        stacked = jnp.stack(pieces, axis=0)
        ordered = [lax.dynamic_index_in_dim(stacked, (tp - t) % n_tp, 0, keepdims=False) for t in range(n_tp)]
        x_rows = lax.dynamic_slice_in_dim(x, tp * rows, rows, 0)
        dy_rows = lax.dynamic_slice_in_dim(dy, tp * rows, rows, 0)
        dx_rows, d_pre = input_grad(ordered, w_all, x_rows, dy_rows, wpre)
        d_hidden = lax.all_gather(dx_rows, "tp", axis=0, tiled=True)

        d_wq = cp_sum(dot(normed, dq, TN))
        d_wkv = cp_sum(dot(normed, d_kv, TN))

        small = jnp.concatenate([jnp.where(tp == 0, d_post[0], 0.0), d_pre[0], dq_gain[0], dk_gain[0]])
        small = small + lax.ppermute(small, "cp", near)
        small = small + lax.ppermute(small, "cp", across)
        small = small + lax.ppermute(small, "tp", [(i, i ^ 1) for i in range(n_tp)])
        small = small + lax.ppermute(small, "tp", [(i, i ^ 2) for i in range(n_tp)])
        d_post, d_pre = small[:dim], small[dim:2 * dim]
        d_qn, d_kn = small[2 * dim:2 * dim + HD], small[2 * dim + HD:]
        kv_cols = kv_heads * HD
        return y[None], d_hidden[None], d_wq, d_wkv[:, :kv_cols], d_wkv[:, kv_cols:], d_wo, d_pre, d_post, d_qn, d_kn

    specs_in = (P('dp', 'cp', None), P('dp', 'cp', None), P(('dp', 'cp')), P(None, 'tp'), P(None, 'tp'), P(None, 'tp'), P('tp', None), P(None), P(None), P(None), P(None))
    specs_out = (P('dp', 'cp', None), P('dp', 'cp', None), P('dp', 'tp'), P('dp', 'tp'), P('dp', 'tp'), P(('dp', 'tp'), None), P('dp'), P('dp'), P('dp'), P('dp'))
    return jax.shard_map(per_device, mesh=mesh, in_specs=specs_in, out_specs=specs_out, check_vma=False)
```

time: 1960 us -> 798 us (0.41)
  waiting for transfers between devices: 1220 us -> 439 us
  matrix products: 437 us -> 24 us
  Pallas kernels: 0 us -> 174 us
  other arithmetic: 136 us -> 78.5 us
  blocking collectives: 44.5 us -> 0 us
  local copies, waits for them, and re-layouts: 86.4 us -> 42.9 us
    psum x3 -> x0, waiting for transfers between devices: 1180 us -> none  [the longest x1 425 us: per_device(): lax.psum(jnp.einsum('bkgqd,kgdm->bqm', out_bf, wo_split, preferred_elemen...]
    dot_general x39 -> x3, matrix products: 437 us -> 24 us  [dot(): return lax.dot_general(a, b, dims, preferred_element_type=F32)]
    ppermute x26 -> x21, waiting for transfers between devices: 37.7 us -> 285 us  [the longest x3 172 us: cp_sum(): keep = keep + lax.ppermute(keep, 'cp', across)]
    pallas_call x0 -> x7, Pallas kernels: none -> 174 us  [the longest x1 54.2 us: attention_bwd(): pl.pallas_call(functools.partial(bwd_kernel, n_cp), name='attention_bwd',...]
    all_gather x0 -> x4, waiting for transfers between devices: none -> 154 us  [the longest x1 112 us: per_device(): out_all = lax.all_gather(out, 'tp', axis=0, tiled=False)]
    reduce_sum x16 -> x0, other arithmetic: 85.2 us -> none  [the longest x4 45.7 us: attend_block(): new_sum = run_sum * factor + jnp.sum(attn_prob, axis=-1)]
    psum x2 -> x0, blocking collectives: 44.5 us -> none  [the longest x1 31.9 us: per_device(): d_qnorm = lax.psum(dq_gain, ('tp', 'cp'))]
    while x40 -> x0, local copies, waits for them, and re-layouts: 39.6 us -> none
  transfers between devices with their start and end apart: 29 -> 25, of which waited for: 9 -> 11; matrix products, arithmetic and copies ran while one was open for 17% -> 16% of each run, Pallas kernels for 0% -> 22%
where the time goes in v1:
time: 798 us; the launch traced here: 791 us
  waiting for transfers between devices  439 us (55%)
  Pallas kernels  174 us (22%)
  other arithmetic  78.5 us (10%)
  local copies, waits for them, and re-layouts  42.9 us (5%)
  matrix products  24 us (3%)
  starting transfers between devices  17.9 us (2%)
  between operations  14.4 us (2%)
    ppermute x3, waiting for transfers between devices, cp_sum(): keep = keep + lax.ppermute(keep, 'cp', across)  172 us
    all_gather x1, waiting for transfers between devices, per_device(): out_all = lax.all_gather(out, 'tp', axis=0, tiled=False)  112 us
    pallas_call x1, Pallas kernels, attention_bwd(): pl.pallas_call(functools.partial(bwd_kernel, n_cp), name='attention_bwd',...  54.2 us
    pallas_call x1, Pallas kernels, post(): pl.pallas_call(post_kernel, name='post', grid=(seq // rows,), in_specs=[p...  46.5 us
    ppermute x3, waiting for transfers between devices, per_device(): lax.ppermute(part, 'tp', [(i, (i + s) % n_tp) for i in range(n_tp)])  44.8 us
    all_gather x1, waiting for transfers between devices, per_device(): lax.all_gather(lax.dynamic_slice_in_dim(w_o, share * o_rows, o_rows, 0),...  42.5 us
    ppermute x1, waiting for transfers between devices, per_device(): dkv_far = lax.ppermute(dkv[1] + got[1], 'cp', across)  32.4 us
    ppermute x1, waiting for transfers between devices, per_device(): kv_far = lax.ppermute(kv_own, 'cp', across)  30.9 us
  transfers between devices with their start and end apart: 25, of which 11 were waited for; matrix products, arithmetic and copies ran while one was open for 16% of the time, Pallas kernels for 22%

profile of v1, /device:TPU:0, one launch (start us, length us, event | category | flops | bytes accessed | tf_op | source)
XLA Modules:
  0.0 791.1 jit_solution(10201611945084681649)
XLA Ops:
  7.2 1.9 constant_dynamic-slice_fusion.9
  9.9 1.9 fusion.2
  13.2 9.5 %project_kv.1 = (bf16[1024,3072]{1,0:T(8,128)(2,1)}, bf16[1024,512]{1,0:T(8,128)(2,1)}, bf16[1024,256]{1,0:T(8,128)(2,1)}) custom-call(bf16[1024,3072]{1,0:T(8,128)(2,1)} %bitcast.48, f32[1,3072]{1,0:T(1,128)} %bitcast.54, bf16[3072,256]{1,0:T(8,128)(2,1)} %wk_ref.1, bf16[3072,256]{1,0:T(8,128)(2,1)} %wv_ref.1, f32[1,128]{1,0:T(1,128)} %bitcast.56, ...), custom_call_target="tpu_custom_call" | custom-call | flops 3221225472 | bytes 15728640 | tf_op jit(solution)/shard_map/project_kv/pallas_call | solution.py:88
  22.7 3.0 collective-permute-start.1
  25.7 30.9 %collective-permute-done.1.rest_2_ = bf16[1024,512]{1,0:T(8,128)(2,1)S(1)} collective-permute-done((bf16[1024,512]{1,0:T(8,128)(2,1)}, bf16[1024,512]{1,0:T(8,128)(2,1)S(1)}, u32[]{:S(2)}, u32[]{:S(2)}) %collective-permute-start.1) | collective-permute-done | bytes 1048608 | tf_op jit(solution)/shard_map/ppermute | solution.py:502
  56.6 11.1 %project_q.1 = (bf16[6,1024,128]{2,1,0:T(8,128)(2,1)}, bf16[6,1024,128]{2,1,0:T(8,128)(2,1)}) custom-call(bf16[1024,3072]{1,0:T(8,128)(2,1)} %get-tuple-element.33.normed_ref, bf16[3072,768]{1,0:T(8,128)(2,1)} %wq_ref.1, f32[1,128]{1,0:T(1,128)} %bitcast.60, f32[1024,128]{1,0:T(8,128)} %get-tuple-element.79.cos_ref, f32[1024,128]{1,0:T(8,128)} %get-tuple-element.80.sin_ref), custom_call_target="tpu_custom_call" | custom-call | flops 4831838208 | bytes 11010048 | tf_op jit(solution)/shard_map/project_q/pallas_call | solution.py:118
  69.1 27.9 %attention_fwd.1 = (bf16[1024,768]{1,0:T(8,128)(2,1)}, f32[2,8,1024]{2,1,0:T(8,128)}) custom-call(s32[1]{0:T(128)} %bitcast.me_ref, bf16[6,1024,128]{2,1,0:T(8,128)(2,1)} %get-tuple-element.34.q_ref, bf16[1024,512]{1,0:T(8,128)(2,1)} %get-tuple-element.35.rest_0_, bf16[1024,512]{1,0:T(8,128)(2,1)} %copy-done.6, bf16[1024,512]{1,0:T(8,128)(2,1)} %copy-done.5, ...), custom_call_target="tpu_custom_call" | custom-call | flops 7247757312 | bytes 6291456 | tf_op jit(solution)/shard_map/attention_fwd/pallas_call | solution.py:219
  97.0 42.5 %all-gather.6.cloned.1.call-done.wall_ref = bf16[3072,3072]{1,0:T(8,128)(2,1)} async-done(((bf16[96,3072]{1,0:T(8,128)(2,1)}), bf16[3072,3072]{1,0:T(8,128)(2,1)}) %all-gather.6.cloned.1.call-update) | async-done | bytes 18874384 | tf_op jit(solution)/shard_map/all_gather | solution.py:494
  142.8 111.6 %all-gather.12.cloned.1.call-done = bf16[4096,768]{1,0:T(8,128)(2,1)} async-done(((bf16[1024,768]{1,0:T(8,128)(2,1)}), bf16[4096,768]{1,0:T(8,128)(2,1)}) %all-gather.12.cloned.1.call-update) | async-done | bytes 6291472 | tf_op jit(solution)/shard_map/all_gather | solution.py:510
  255.0 46.5 %post.1 = (bf16[1024,3072]{1,0:T(8,128)(2,1)}, bf16[1024,3072]{1,0:T(8,128)(2,1)}, bf16[6,1024,128]{2,1,0:T(8,128)(2,1)}, f32[8,3072]{1,0:T(8,128)}) custom-call(bf16[4,1024,768]{2,1,0:T(8,128)(2,1)} %bitcast.58, bf16[3072,3072]{1,0:T(8,128)(2,1)} %all-gather.6.cloned.1.call-done.wall_ref, bf16[768,3072]{1,0:T(8,128)(2,1)} %wmine_ref.1, ...), custom_call_target="tpu_custom_call" | custom-call | flops 24159191040 | bytes 48758784 | tf_op jit(solution)/shard_map/post/pallas_call | solution.py:368
  301.5 10.3 %fusion.6 = f32[768,3072]{1,0:T(8,128)} fusion(bf16[1024,768]{1,0:T(8,128)(2,1)S(1)} %copy-done.3, bf16[1024,3072]{1,0:T(8,128)(2,1)} %get-tuple-element.40), kind=kOutput, calls=%fused_computation.51 | convolution fusion | flops 4831838208 | bytes 17301504 | tf_op jit(solution)/shard_map/dot_general | solution.py:25
  311.9 54.2 %attention_bwd.1 = (bf16[1024,768]{1,0:T(8,128)(2,1)}, f32[4,2,2,1024,128]{4,3,2,1,0:T(8,128)}, f32[8,128]{1,0:T(8,128)}) custom-call(s32[1]{0:T(128)} %bitcast.me_ref, bf16[6,1024,128]{2,1,0:T(8,128)(2,1)} %get-tuple-element.34.q_ref, bf16[6,1024,128]{2,1,0:T(8,128)(2,1)} %get-tuple-element.42.do_ref, bf16[1024,768]{1,0:T(8,128)(2,1)} %get-tuple-element.37.o_ref, ...), custom_call_target="tpu_custom_call" | custom-call | flops 18119393280 | bytes 12582912 | tf_op jit(solution)/shard_map/attention_bwd/pallas_call | solution.py:326
  366.1 7.7 fusion.7
  373.9 2.6 constant_dynamic-slice_fusion.2
  376.4 4.4 copy-done.1
  382.2 2.3 slice.39
  384.5 5.1 constant_dynamic-slice_fusion
  390.1 5.1 collective-permute-done.3.near_ref
  395.2 3.7 fusion.1
  400.4 6.6 dynamic-slice_add_fusion.1
  407.6 6.9 dynamic-slice_add_fusion
  417.5 32.4 %collective-permute-done.4.far_ref = f32[2,2,1024,128]{3,2,1,0:T(8,128)} collective-permute-done((f32[2,2,1024,128]{3,2,1,0:T(8,128)}, f32[2,2,1024,128]{3,2,1,0:T(8,128)}, u32[]{:S(2)}, u32[]{:S(2)}) %collective-permute-start.4) | collective-permute-done | bytes 2097184 | tf_op jit(solution)/shard_map/ppermute | solution.py:532
  449.8 5.5 key_back.1
  455.4 5.9 fusion.8
  461.3 2.0 constant_dynamic-slice_fusion.1
  466.8 2.4 collective-permute-start.6
  469.2 15.6 %collective-permute-done.5 = bf16[256,1280]{1,0:T(8,128)(2,1)S(1)} collective-permute-done((bf16[256,1280]{1,0:T(8,128)(2,1)}, bf16[256,1280]{1,0:T(8,128)(2,1)S(1)}, u32[]{:S(2)}, u32[]{:S(2)}) %collective-permute-start.5) | collective-permute-done | bytes 655392 | tf_op jit(solution)/shard_map/ppermute | solution.py:541
  485.5 2.7 dynamic-slice_bitcast_fusion.refs_6_
  488.2 2.7 dynamic-slice_bitcast_fusion.1.refs_5_
  490.8 20.9 %collective-permute-done.6 = bf16[256,1280]{1,0:T(8,128)(2,1)S(1)} collective-permute-done((bf16[256,1280]{1,0:T(8,128)(2,1)}, bf16[256,1280]{1,0:T(8,128)(2,1)S(1)}, u32[]{:S(2)}, u32[]{:S(2)}) %collective-permute-start.6) | collective-permute-done | bytes 655392 | tf_op jit(solution)/shard_map/ppermute | solution.py:541
  511.7 8.2 %collective-permute-done.7 = bf16[256,1280]{1,0:T(8,128)(2,1)S(1)} collective-permute-done((bf16[256,1280]{1,0:T(8,128)(2,1)S(1)}, bf16[256,1280]{1,0:T(8,128)(2,1)S(1)}, u32[]{:S(2)}, u32[]{:S(2)}) %collective-permute-start.7) | collective-permute-done | bytes 655392 | tf_op jit(solution)/shard_map/ppermute | solution.py:541
  520.3 30.7 %collective-permute-done.9 = f32[1536,768]{1,0:T(8,128)} collective-permute-done((f32[1536,768]{1,0:T(8,128)}, f32[1536,768]{1,0:T(8,128)}, u32[]{:S(2)}, u32[]{:S(2)}) %collective-permute-start.9) | collective-permute-done | bytes 4718624 | tf_op jit(solution)/shard_map/ppermute | solution.py:521
  550.9 6.6 add.154
  559.1 19.6 %input_grad.1 = (bf16[256,3072]{1,0:T(8,128)(2,1)}, f32[8,3072]{1,0:T(8,128)}) custom-call(bf16[256,1280]{1,0:T(8,128)(2,1)} %get-tuple-element.67.refs_0_, bf16[256,1280]{1,0:T(8,128)(2,1)} %get-tuple-element.66.refs_1_, bf16[256,1280]{1,0:T(8,128)(2,1)} %get-tuple-element.65.refs_2_, bf16[256,1280]{1,0:T(8,128)(2,1)} %get-tuple-element.64.refs_3_, ...), custom_call_target="tpu_custom_call" | custom-call | flops 8053063680 | bytes 31457280 | tf_op jit(solution)/shard_map/input_grad/pallas_call | solution.py:460
  578.7 73.1 %collective-permute-done.15 = f32[384,3072]{1,0:T(8,128)} collective-permute-done((f32[384,3072]{1,0:T(8,128)}, f32[384,3072]{1,0:T(8,128)}, u32[]{:S(2)}, u32[]{:S(2)}) %collective-permute-start.15) | collective-permute-done | bytes 4718624 | tf_op jit(solution)/shard_map/ppermute | solution.py:521
  651.8 7.0 add.160
  658.8 3.6 dynamic-slice_add_fusion.2
  665.1 67.9 %collective-permute-done.12 = f32[1536,512]{1,0:T(8,128)} collective-permute-done((f32[1536,512]{1,0:T(8,128)S(1)}, f32[1536,512]{1,0:T(8,128)}, u32[]{:S(2)}, u32[]{:S(2)}) %collective-permute-start.12) | collective-permute-done | bytes 3145760 | tf_op jit(solution)/shard_map/ppermute | solution.py:521
  733.0 4.3 add.156
  737.3 4.4 broadcast_select_fusion.3
  741.7 9.2 %broadcast_select_fusion.1 = (f32[384,3072]{1,0:T(8,128)}, f32[384,3072]{1,0:T(8,128)}) fusion(f32[384,3072]{1,0:T(8,128)} %add.160, f32[384,3072]{1,0:T(8,128)} %collective-permute-done.16, pred[]{:T(512)S(6)} %eq.22), kind=kLoop, calls=%fused_computation.11 | loop fusion | flops 2359296 | bytes 18874368 | tf_op jit(solution)/shard_map/jit(_where)/select_n | solution.py:523
  752.3 8.7 %pad_maximum_fusion.1 = f32[768,3072]{1,0:T(8,128)} fusion(f32[384,3072]{1,0:T(8,128)} %get-tuple-element.57, f32[384,3072]{1,0:T(8,128)} %get-tuple-element.56), kind=kLoop, calls=%fused_computation.1 | loop fusion | flops 2359296 | bytes 18874368 | tf_op jit(solution)/shard_map/concatenate | solution.py:525
  761.5 4.3 pad_maximum_fusion
  765.8 1.8 collective-permute-start.19
  767.6 3.8 broadcast_select_fusion.4
  771.4 2.5 collective-permute-start.20
  773.9 3.2 pad_maximum_fusion.2
  778.2 5.9 copy.23
  (76 shorter events, 26.0 us)
Async XLA Ops:
  7.2 132.4 %all-gather.6.cloned.1.call-start = ((), (), s32[]{:S(2)}) async-start(), calls=%async_computation | async-start | bytes 19464192 | tf_op jit(solution)/shard_map/all_gather | solution.py:494
  9.2 245.3 %all-gather.12.cloned.1.call-start = ((), (), s32[]{:S(2)}) async-start(), calls=%async_computation.3 | async-start | bytes 7864320 | tf_op jit(solution)/shard_map/all_gather | solution.py:510
  22.7 33.9 %collective-permute-start.1 = (bf16[1024,512]{1,0:T(8,128)(2,1)}, bf16[1024,512]{1,0:T(8,128)(2,1)S(1)}, u32[]{:S(2)}, u32[]{:S(2)}) collective-permute-start(bf16[1024,512]{1,0:T(8,128)(2,1)} %get-tuple-element.35.rest_0_), channel_id=1, source_target_pairs={{0,2},{1,3},{2,0},{3,1},{4,6},{5,7},{6,4},{7,5},{8,10},{9,11},{10,... | collective-permute-start | bytes 3145736 | tf_op jit(solution)/shard_map/ppermute | solution.py:502
  25.7 42.0 %collective-permute-start = (bf16[1024,512]{1,0:T(8,128)(2,1)}, bf16[1024,512]{1,0:T(8,128)(2,1)S(1)}, u32[]{:S(2)}, u32[]{:S(2)}) collective-permute-start(bf16[1024,512]{1,0:T(8,128)(2,1)} %get-tuple-element.35.rest_0_), channel_id=1, source_target_pairs={{0,1},{1,0},{2,3},{3,2},{4,5},{5,4},{6,7},{7,6},{8,9},{9,8},{10,11... | collective-permute-start | bytes 3145736 | tf_op jit(solution)/shard_map/ppermute | solution.py:503
  56.6 11.1 %copy-start.5 = (bf16[1024,512]{1,0:T(8,128)(2,1)}, bf16[1024,512]{1,0:T(8,128)(2,1)S(1)}, u32[]{:S(2)}) copy-start(bf16[1024,512]{1,0:T(8,128)(2,1)S(1)} %collective-permute-done.1.rest_2_) | copy-start | bytes 3145732
  56.6 11.1 %collective-permute-start.2 = (bf16[1024,512]{1,0:T(8,128)(2,1)S(1)}, bf16[1024,512]{1,0:T(8,128)(2,1)S(1)}, u32[]{:S(2)}, u32[]{:S(2)}) collective-permute-start(bf16[1024,512]{1,0:T(8,128)(2,1)S(1)} %collective-permute-done.1.rest_2_), channel_id=1, source_target_pairs={{0,1},{1,0},{2,3},{3,2},{4,5},{5,4},{6,7},{7,6},{8,9},{9,8},{10,11... | collective-permute-start | bytes 3145736 | tf_op jit(solution)/shard_map/ppermute | solution.py:504
  67.7 1.0 copy-start.6
  67.7 1.3 copy-start.7
  139.6 419.5 %all-gather.8.cloned.1.call-start = ((), (), s32[]{:S(2)}) async-start(), calls=%async_computation.1 | async-start | bytes 32440320 | tf_op jit(solution)/shard_map/all_gather | solution.py:513
  254.5 523.7 %all-gather.10.cloned.1.call-start = ((), (), s32[]{:S(2)}) async-start(), calls=%async_computation.2 | async-start | bytes 7864320 | tf_op jit(solution)/shard_map/all_gather | solution.py:547
  255.0 46.5 %copy-start.3 = (bf16[1024,768]{1,0:T(8,128)(2,1)S(1)}, bf16[1024,768]{1,0:T(8,128)(2,1)}, u32[]{:S(2)}) copy-start(bf16[1024,768]{1,0:T(8,128)(2,1)} %get-tuple-element.37.o_ref) | copy-start | bytes 4718596
  373.8 7.0 copy-start.1
  373.8 8.4 %copy-start = (f32[4,2,2,1024,128]{4,3,2,1,0:T(8,128)S(1)}, f32[4,2,2,1024,128]{4,3,2,1,0:T(8,128)}, u32[]{:S(2)}) copy-start(f32[4,2,2,1024,128]{4,3,2,1,0:T(8,128)} %get-tuple-element.46.own_ref) | copy-start | bytes 25165828
  380.9 19.6 %collective-permute-start.8 = (f32[1536,768]{1,0:T(8,128)}, f32[1536,768]{1,0:T(8,128)}, u32[]{:S(2)}, u32[]{:S(2)}) collective-permute-start(f32[1536,768]{1,0:T(8,128)} %constant_dynamic-slice_fusion.2), channel_id=1, source_target_pairs={{0,1},{1,0},{2,3},{3,2},{4,5},{5,4},{6,7},{7,6},{8,9},{9,8},{10,11... | collective-permute-start | bytes 14155784 | tf_op jit(solution)/shard_map/ppermute | solution.py:520
  384.5 10.7 %collective-permute-start.3 = (f32[2,2,2,1024,128]{4,3,2,1,0:T(8,128)}, f32[2,2,2,1024,128]{4,3,2,1,0:T(8,128)}, u32[]{:S(2)}, u32[]{:S(2)}) collective-permute-start(f32[2,2,2,1024,128]{4,3,2,1,0:T(8,128)} %slice.39), channel_id=1, source_target_pairs={{0,1},{1,0},{2,3},{3,2},{4,5},{5,4},{6,7},{7,6},{8,9},{9,8},{10,11... | collective-permute-start | bytes 12582920 | tf_op jit(solution)/shard_map/ppermute | solution.py:531
  389.6 18.0 %collective-permute-start.14 = (f32[384,3072]{1,0:T(8,128)}, f32[384,3072]{1,0:T(8,128)}, u32[]{:S(2)}, u32[]{:S(2)}) collective-permute-start(f32[384,3072]{1,0:T(8,128)} %constant_dynamic-slice_fusion), channel_id=1, source_target_pairs={{0,1},{1,0},{2,3},{3,2},{4,5},{5,4},{6,7},{7,6},{8,9},{9,8},{10,11... | collective-permute-start | bytes 14155784 | tf_op jit(solution)/shard_map/ppermute | solution.py:520
  398.9 50.9 %collective-permute-start.4 = (f32[2,2,1024,128]{3,2,1,0:T(8,128)}, f32[2,2,1024,128]{3,2,1,0:T(8,128)}, u32[]{:S(2)}, u32[]{:S(2)}) collective-permute-start(f32[2,2,1024,128]{3,2,1,0:T(8,128)} %fusion.1), channel_id=1, source_target_pairs={{0,2},{1,3},{2,0},{3,1},{4,6},{5,7},{6,4},{7,5},{8,10},{9,11},{10,... | collective-permute-start | bytes 6291464 | tf_op jit(solution)/shard_map/ppermute | solution.py:532
  407.0 143.9 %collective-permute-start.9 = (f32[1536,768]{1,0:T(8,128)}, f32[1536,768]{1,0:T(8,128)}, u32[]{:S(2)}, u32[]{:S(2)}) collective-permute-start(f32[1536,768]{1,0:T(8,128)} %dynamic-slice_add_fusion.1), channel_id=1, source_target_pairs={{0,2},{1,3},{2,0},{3,1},{4,6},{5,7},{6,4},{7,5},{8,10},{9,11},{10,... | collective-permute-start | bytes 14155784 | tf_op jit(solution)/shard_map/ppermute | solution.py:521
  414.5 237.3 %collective-permute-start.15 = (f32[384,3072]{1,0:T(8,128)}, f32[384,3072]{1,0:T(8,128)}, u32[]{:S(2)}, u32[]{:S(2)}) collective-permute-start(f32[384,3072]{1,0:T(8,128)} %dynamic-slice_add_fusion), channel_id=1, source_target_pairs={{0,2},{1,3},{2,0},{3,1},{4,6},{5,7},{6,4},{7,5},{8,10},{9,11},{10,... | collective-permute-start | bytes 14155784 | tf_op jit(solution)/shard_map/ppermute | solution.py:521
  461.3 4.0 copy-start.2
  461.3 2.0 copy-start.4
  463.3 195.5 %collective-permute-start.11 = (f32[1536,512]{1,0:T(8,128)}, f32[1536,512]{1,0:T(8,128)}, u32[]{:S(2)}, u32[]{:S(2)}) collective-permute-start(f32[1536,512]{1,0:T(8,128)} %constant_dynamic-slice_fusion.1), channel_id=1, source_target_pairs={{0,1},{1,0},{2,3},{3,2},{4,5},{5,4},{6,7},{7,6},{8,9},{9,8},{10,11... | collective-permute-start | bytes 9437192 | tf_op jit(solution)/shard_map/ppermute | solution.py:520
  465.3 19.5 %collective-permute-start.5 = (bf16[256,1280]{1,0:T(8,128)(2,1)}, bf16[256,1280]{1,0:T(8,128)(2,1)S(1)}, u32[]{:S(2)}, u32[]{:S(2)}) collective-permute-start(bf16[256,1280]{1,0:T(8,128)(2,1)} %get-tuple-element.71), channel_id=1, source_target_pairs={{0,4},{4,8},{8,12},{12,0},{1,5},{5,9},{9,13},{13,1},{2,6},{6,10},{... | collective-permute-start | bytes 1966088 | tf_op jit(solution)/shard_map/ppermute | solution.py:541
  466.8 44.9 %collective-permute-start.6 = (bf16[256,1280]{1,0:T(8,128)(2,1)}, bf16[256,1280]{1,0:T(8,128)(2,1)S(1)}, u32[]{:S(2)}, u32[]{:S(2)}) collective-permute-start(bf16[256,1280]{1,0:T(8,128)(2,1)} %get-tuple-element.70), channel_id=1, source_target_pairs={{0,8},{4,12},{8,0},{12,4},{1,9},{5,13},{9,1},{13,5},{2,10},{6,14},... | collective-permute-start | bytes 1966088 | tf_op jit(solution)/shard_map/ppermute | solution.py:541
  484.9 35.1 %collective-permute-start.7 = (bf16[256,1280]{1,0:T(8,128)(2,1)S(1)}, bf16[256,1280]{1,0:T(8,128)(2,1)S(1)}, u32[]{:S(2)}, u32[]{:S(2)}) collective-permute-start(bf16[256,1280]{1,0:T(8,128)(2,1)S(1)} %get-tuple-element.69), channel_id=1, source_target_pairs={{0,12},{4,0},{8,4},{12,8},{1,13},{5,1},{9,5},{13,9},{2,14},{6,2},{... | collective-permute-start | bytes 1966088 | tf_op jit(solution)/shard_map/ppermute | solution.py:541
  557.5 179.8 %collective-permute-start.10 = (f32[1536,768]{1,0:T(8,128)}, f32[1536,768]{1,0:T(8,128)}, u32[]{:S(2)}, u32[]{:S(2)}) collective-permute-start(f32[1536,768]{1,0:T(8,128)} %add.154), channel_id=1, source_target_pairs={{0,1},{1,0},{2,3},{3,2},{4,5},{5,4},{6,7},{7,6},{8,9},{9,8},{10,11... | collective-permute-start | bytes 14155784 | tf_op jit(solution)/shard_map/ppermute | solution.py:522
  658.8 82.9 %collective-permute-start.16 = (f32[384,3072]{1,0:T(8,128)}, f32[384,3072]{1,0:T(8,128)}, u32[]{:S(2)}, u32[]{:S(2)}) collective-permute-start(f32[384,3072]{1,0:T(8,128)} %add.160), channel_id=1, source_target_pairs={{0,1},{1,0},{2,3},{3,2},{4,5},{5,4},{6,7},{7,6},{8,9},{9,8},{10,11... | collective-permute-start | bytes 14155784 | tf_op jit(solution)/shard_map/ppermute | solution.py:522
  662.4 70.6 %collective-permute-start.12 = (f32[1536,512]{1,0:T(8,128)S(1)}, f32[1536,512]{1,0:T(8,128)}, u32[]{:S(2)}, u32[]{:S(2)}) collective-permute-start(f32[1536,512]{1,0:T(8,128)S(1)} %dynamic-slice_add_fusion.2), channel_id=1, source_target_pairs={{0,2},{1,3},{2,0},{3,1},{4,6},{5,7},{6,4},{7,5},{8,10},{9,11},{10,... | collective-permute-start | bytes 9437192 | tf_op jit(solution)/shard_map/ppermute | solution.py:521
  737.3 30.3 %collective-permute-start.13 = (f32[1536,512]{1,0:T(8,128)}, f32[1536,512]{1,0:T(8,128)}, u32[]{:S(2)}, u32[]{:S(2)}) collective-permute-start(f32[1536,512]{1,0:T(8,128)} %add.156), channel_id=1, source_target_pairs={{0,1},{1,0},{2,3},{3,2},{4,5},{5,4},{6,7},{7,6},{8,9},{9,8},{10,11... | collective-permute-start | bytes 9437192 | tf_op jit(solution)/shard_map/ppermute | solution.py:522
  751.8 9.3 %collective-permute-start.17 = (f32[6400]{0:T(1024)S(1)}, f32[6400]{0:T(1024)S(1)}, u32[]{:S(2)}, u32[]{:S(2)}) collective-permute-start(f32[6400]{0:T(1024)S(1)} %pad_maximum_fusion.7), channel_id=1, source_target_pairs={{0,1},{1,0},{2,3},{3,2},{4,5},{5,4},{6,7},{7,6},{8,9},{9,8},{10,11... | collective-permute-start | bytes 76808 | tf_op jit(solution)/shard_map/ppermute | solution.py:553
  761.1 4.8 collective-permute-start.18
  765.8 5.6 collective-permute-start.19
  771.4 5.7 collective-permute-start.20
Sparse Core Ops, SparseCore 0:
  11.5 128.0 all-gather.5
  141.1 113.2 all-gather.11
  257.4 185.8 all-gather.7
  578.9 115.0 all-gather.9
